TPU v7x, 32 devices: a whole 2x2x4 slice. The times are simulated.
32 devices in a mesh: leaf: 8 (over y, x, core), rhs: 4 (over z).
Axes of the slice: x: 2, y: 2, z: 4, core: 2. Of those that a mesh axis runs over, the one named last changes fastest.
Arguments:
- charges: bfloat16 [65536, 2048], P(('leaf', 'rhs')), may hold values from -6 to 6
- leaf_coef: bfloat16 [128, 256, 512], P(('leaf', 'rhs')), may hold values from -0.25 to 0.25
- leaf_rows: int32 [128, 256], P(('leaf', 'rhs')), may hold values from 0 to 511, as said below
- local_interp: bfloat16 [120, 256, 512], P('leaf'), may hold values from -0.25 to 0.25
- top_interp: bfloat16 [1792, 512], P('leaf'), may hold values from -0.25 to 0.25
Outputs:
- subtree_skel: bfloat16 [2048, 2048], P('leaf', 'rhs')
- top_skel: bfloat16 [1792, 2048], P('leaf', 'rhs')
Inputs may be any that keep to these rules, and one draw needn't show every extreme that they name: `leaf_rows`: each row holds 256 distinct positions.
All inputs are finite; a program needn't handle non-finite values.
Results may differ from a plain program's by a relative error of at most 0.012.
Values may be sent and summed in bfloat16 or wider, within the bound.
A program may use at most 64 MiB of HBM per device.

v0:
```python
import jax
import jax.numpy as jnp
from jax import lax
from jax.sharding import PartitionSpec as P


def partner(block, axis, distance):
    count = lax.axis_size(axis)
    route = []
    for low in range(count):
        high = low | 1 << distance
        if high != low and high < count:
            route += [(low, high), (high, low)]
    return lax.ppermute(block, axis, route)


def pick_rows(block, chosen):
    return block[chosen]


def pair_up(own_part, other_part, bitnum, leaf_pos):
    lower_half = leaf_pos >> bitnum & 1 == 0
    return jnp.where(
        lower_half,
        jnp.concatenate([own_part, other_part], 0),
        jnp.concatenate([other_part, own_part], 0),
    )


def with_sibling(child, bitnum, leaf_pos):
    other_part = partner(child, "leaf", bitnum)
    return pair_up(child, other_part, bitnum, leaf_pos)


def local(charges, leaf_coef, leaf_rows, local_interp, top_interp):
    rhs_count = lax.axis_size("rhs")
    leaves_here = leaf_coef.shape[0]
    skel_size = leaf_coef.shape[1]
    leaf_size = leaf_coef.shape[2]
    leaves_total = leaves_here * rhs_count
    all_cols = charges.shape[1]
    rhs_pos = lax.axis_index("rhs")
    points = charges.reshape(leaves_here, leaf_size, all_cols)
    picked = jax.vmap(pick_rows)(points, leaf_rows).astype(jnp.float32)
    mixed = jnp.einsum("nsm,nmc->nsc", leaf_coef, points, preferred_element_type=jnp.float32)
    skeleton = (picked + mixed).astype(jnp.bfloat16)

    def climb(skeleton, level, first_node):
        node_count = skeleton.shape[0] // 2
        offset = leaves_total - (leaves_total >> level - 1) + first_node
        matrices = lax.dynamic_slice_in_dim(local_interp, offset, node_count, 0)
        stacked = skeleton.reshape(node_count, 2 * skel_size, skeleton.shape[2])
        return jnp.einsum(
            "nij,njc->nic", matrices, stacked, preferred_element_type=jnp.float32
        ).astype(jnp.bfloat16)

    early = leaves_here.bit_length() - 1
    for level in range(1, early + 1):
        skeleton = climb(skeleton, level, rhs_pos * (leaves_here >> level))
    skeleton = lax.all_to_all(skeleton, "rhs", split_axis=2, concat_axis=0, tiled=True)
    tree_depth = leaves_total.bit_length() - 1
    for level in range(early + 1, tree_depth + 1):
        skeleton = climb(skeleton, level, 0)
    root = skeleton[0]
    leaf_count = lax.axis_size("leaf")
    top_levels = leaf_count.bit_length() - 1
    leaf_pos = lax.axis_index("leaf")
    pieces = []
    held = root
    for level in range(1, top_levels + 1):
        row_count = skel_size >> level
        offset = skel_size - (skel_size >> level - 1)
        child = held
        for bitnum in range(level - 1):
            other_part = partner(child, "leaf", bitnum)
            child = pair_up(child, other_part, bitnum, leaf_pos)
        stacked = with_sibling(child, level - 1, leaf_pos)
        matrices = top_interp[offset : offset + row_count]
        held = jnp.dot(matrices, stacked, preferred_element_type=jnp.float32).astype(jnp.bfloat16)
        pieces.append(held)
    top_skel = jnp.concatenate(pieces, axis=0)
    return (root, top_skel)


def solution(mesh):
    placed = (
        P(("leaf", "rhs"), None),
        P(("leaf", "rhs"), None, None),
        P(("leaf", "rhs"), None),
        P("leaf", None, None),
        P("leaf", None),
    )
    return jax.shard_map(
        local,
        mesh=mesh,
        in_specs=placed,
        out_specs=(P("leaf", "rhs"), P("leaf", "rhs")),
        check_vma=False,
    )
```

profile of v0, /device:TPU:0, one launch (start us, length us, event | category | flops | bytes accessed | tf_op | source)
XLA Modules:
  0.0 128.6 jit_solution(11244644073061906736)
XLA Ops:
  0.6 0.8 fusion.37
  1.4 25.4 %gather_fusion = bf16[1024,2048]{1,0:T(8,128)(2,1)} fusion(bf16[4,512,2048]{2,1,0:T(8,128)(2,1)} %bitcast.46, s32[1024]{0:T(1024)S(1)} %bitcast.48), kind=kCustom, calls=%fused_computation | custom fusion | bytes 8396800 | tf_op jit(solution)/shard_map/vmap()/gather | solution.py:18
  26.9 8.9 %fusion = bf16[4,256,2048]{2,1,0:T(8,128)(2,1)} fusion(bf16[4,256,2048]{2,1,0:T(8,128)(2,1)} %bitcast.49, bf16[4,256,512]{2,1,0:T(8,128)(2,1)S(1)} %copy-done, bf16[4,512,2048]{2,1,0:T(8,128)(2,1)} %bitcast.47), kind=kOutput, calls=%fused_computation.2 | convolution fusion | flops 2153775104 | bytes 17825792 | tf_op jit(solution)/shard_map/nsm,nmc->nsc/dot_general | solution.py:45
  35.8 3.6 %convolution_convert_fusion = bf16[2,256,2048]{2,1,0:T(8,128)(2,1)S(1)} fusion(bf16[2,512,2048]{2,1,0:T(8,128)(2,1)} %bitcast.50, bf16[15,256,512]{2,1,0:T(8,128)(2,1)} %param.8, s32[]{:T(128)S(6)} %select_n.52), kind=kOutput, calls=%fused_computation.3 | convolution fusion | flops 1074790400 | bytes 6815748 | tf_op jit(solution)/shard_map/nij,njc->nic/dot_general | solution.py:53
  39.4 2.7 %fusion.1 = bf16[1,256,2048]{2,1,0:T(8,128)(2,1)} fusion(bf16[512,2048]{1,0:T(8,128)(2,1)S(1)} %bitcast.52, bf16[15,256,512]{2,1,0:T(8,128)(2,1)} %param.8, s32[]{:T(128)S(6)} %select_n.51), kind=kOutput, calls=%fused_computation.5 | convolution fusion | flops 537395200 | bytes 3407876 | tf_op jit(solution)/shard_map/nij,njc->nic/dot_general | solution.py:53
  42.1 4.6 %copy.10 = bf16[1,256,2048]{1,0,2:T(2,128)(2,1)S(1)} copy(bf16[1,256,2048]{2,1,0:T(8,128)(2,1)} %fusion.1) | data formatting | bytes 2097152 | tf_op jit(solution)/shard_map/convert_element_type | solution.py:55
  47.2 11.6 %reduce = bf16[2048,256]{1,0:T(8,128)(2,1)} reduce(bf16[2048,1,256]{2,1,0:T(2,128)(2,1)S(1)} %bitcast.53, bf16[]{:T(256)} %broadcast.24), dimensions={1}, to_apply=%bitcast.38.reduce_sub_computation | reduce | bytes 2097154
  58.8 2.2 %reshape.54 = bf16[4,2,65536]{2,1,0:T(2,128)(2,1)S(1)} reshape(bf16[2048,256]{1,0:T(8,128)(2,1)} %reduce) | data formatting | bytes 2097152
  60.9 32.0 %all_to_all.15 = bf16[4,2,65536]{2,1,0:T(2,128)(2,1)} all-to-all(bf16[4,2,65536]{2,1,0:T(2,128)(2,1)S(1)} %reshape.54), channel_id=1, replica_groups=mesh['leaf'=8,'rhs'=4] {'rhs'}, dimensions={0} | all-to-all | bytes 2097152 | tf_op jit(solution)/shard_map/all_to_all | solution.py:60
  92.9 2.6 %reshape.55 = bf16[2048,1,256]{2,1,0:T(2,128)(2,1)S(1)} reshape(bf16[4,2,65536]{2,1,0:T(2,128)(2,1)} %all_to_all.15) | data formatting | bytes 2097152
  95.6 1.1 copy.12
  96.7 1.5 %copy.11 = bf16[4,1,256,512]{3,2,0,1:T(8,128)(2,1)S(1)} copy(bf16[4,1,256,512]{2,3,0,1:T(8,128)(2,1)} %bitcast.54) | data formatting | bytes 2097152 | tf_op jit(solution)/shard_map/all_to_all | solution.py:60
  98.2 1.5 %convolution_convert_fusion.2 = bf16[2,512,256]{1,2,0:T(8,128)(2,1)S(1)} fusion(bf16[2,512,512]{2,1,0:T(8,128)(2,1)S(1)} %bitcast.55, bf16[15,256,512]{2,1,0:T(8,128)(2,1)} %param.8), kind=kOutput, calls=%fused_computation.6 | convolution fusion | flops 268697600 | bytes 2097152 | tf_op jit(solution)/shard_map/nij,njc->nic/dot_general | solution.py:53
  99.7 1.2 fusion.2
  101.0 1.5 %collective-permute-done = bf16[256,512]{1,0:T(8,128)(2,1)S(1)} collective-permute-done((bf16[256,512]{1,0:T(8,128)(2,1)S(1)}, bf16[256,512]{1,0:T(8,128)(2,1)S(1)}, u32[]{:S(2)}, u32[]{:S(2)}) %collective-permute-start) | collective-permute-done | bytes 262176 | tf_op jit(solution)/shard_map/ppermute | solution.py:14
  103.1 1.2 collective-permute-done.1
  104.3 1.6 %collective-permute-start.2 = (bf16[256,512]{1,0:T(8,128)(2,1)S(1)}, bf16[256,512]{1,0:T(8,128)(2,1)S(1)}, u32[]{:S(2)}, u32[]{:S(2)}) collective-permute-start(bf16[256,512]{1,0:T(8,128)(2,1)S(1)} %maximum_select_fusion.6), channel_id=1, source_target_pairs={{0,8},{8,0},{4,12},{12,4},{16,24},{24,16},{20,28},{28,20},{1,9},{9... | collective-permute-start | bytes 786440 | tf_op jit(solution)/shard_map/ppermute | solution.py:14
  105.9 6.9 %collective-permute-done.2 = bf16[256,512]{1,0:T(8,128)(2,1)S(1)} collective-permute-done((bf16[256,512]{1,0:T(8,128)(2,1)S(1)}, bf16[256,512]{1,0:T(8,128)(2,1)S(1)}, u32[]{:S(2)}, u32[]{:S(2)}) %collective-permute-start.2) | collective-permute-done | bytes 262176 | tf_op jit(solution)/shard_map/ppermute | solution.py:14
  113.1 1.2 collective-permute-done.3
  114.4 1.6 %collective-permute-start.4 = (bf16[128,512]{1,0:T(8,128)(2,1)S(1)}, bf16[128,512]{1,0:T(8,128)(2,1)S(1)}, u32[]{:S(2)}, u32[]{:S(2)}) collective-permute-start(bf16[128,512]{1,0:T(8,128)(2,1)S(1)} %maximum_select_fusion.8), channel_id=1, source_target_pairs={{0,8},{8,0},{4,12},{12,4},{16,24},{24,16},{20,28},{28,20},{1,9},{9... | collective-permute-start | bytes 393224 | tf_op jit(solution)/shard_map/ppermute | solution.py:14
  115.9 4.1 %collective-permute-done.4 = bf16[128,512]{1,0:T(8,128)(2,1)S(1)} collective-permute-done((bf16[128,512]{1,0:T(8,128)(2,1)S(1)}, bf16[128,512]{1,0:T(8,128)(2,1)S(1)}, u32[]{:S(2)}, u32[]{:S(2)}) %collective-permute-start.4) | collective-permute-done | bytes 131104 | tf_op jit(solution)/shard_map/ppermute | solution.py:14
  120.1 1.6 %collective-permute-start.5 = (bf16[256,512]{1,0:T(8,128)(2,1)S(1)}, bf16[256,512]{1,0:T(8,128)(2,1)S(1)}, u32[]{:S(2)}, u32[]{:S(2)}) collective-permute-start(bf16[256,512]{1,0:T(8,128)(2,1)S(1)} %maximum_select_fusion.7), channel_id=1, source_target_pairs={{0,16},{16,0},{4,20},{20,4},{8,24},{24,8},{12,28},{28,12},{1,17},{... | collective-permute-start | bytes 786440 | tf_op jit(solution)/shard_map/ppermute | solution.py:14
  121.6 6.0 %collective-permute-done.5 = bf16[256,512]{1,0:T(8,128)(2,1)S(1)} collective-permute-done((bf16[256,512]{1,0:T(8,128)(2,1)S(1)}, bf16[256,512]{1,0:T(8,128)(2,1)S(1)}, u32[]{:S(2)}, u32[]{:S(2)}) %collective-permute-start.5) | collective-permute-done | bytes 262176 | tf_op jit(solution)/shard_map/ppermute | solution.py:14
  127.9 0.7 pad_maximum_fusion
  (17 shorter events, 1.8 us)
Async XLA Ops:
  0.6 26.2 %copy-start = (bf16[4,256,512]{2,1,0:T(8,128)(2,1)S(1)}, bf16[4,256,512]{2,1,0:T(8,128)(2,1)}, u32[]{:S(2)}) copy-start(bf16[4,256,512]{2,1,0:T(8,128)(2,1)} %param.6) | copy-start | bytes 3145732
  95.5 7.0 %copy-start.2 = (bf16[224,512]{1,0:T(8,128)(2,1)S(1)}, bf16[224,512]{1,0:T(8,128)(2,1)}, u32[]{:S(2)}) copy-start(bf16[224,512]{1,0:T(8,128)(2,1)} %param.9) | copy-start | bytes 688132
  100.9 27.7 %copy-start.1 = (bf16[256,512]{1,0:T(8,128)(2,1)}, bf16[256,512]{1,0:T(8,128)(2,1)S(1)}, u32[]{:S(2)}) copy-start(bf16[256,512]{1,0:T(8,128)(2,1)S(1)} %fusion.2) | copy-start | bytes 786436
  101.0 1.6 %collective-permute-start = (bf16[256,512]{1,0:T(8,128)(2,1)S(1)}, bf16[256,512]{1,0:T(8,128)(2,1)S(1)}, u32[]{:S(2)}, u32[]{:S(2)}) collective-permute-start(bf16[256,512]{1,0:T(8,128)(2,1)S(1)} %fusion.2), channel_id=1, source_target_pairs={{0,4},{4,0},{8,12},{12,8},{16,20},{20,16},{24,28},{28,24},{1,5},{5... | collective-permute-start | bytes 786440 | tf_op jit(solution)/shard_map/ppermute | solution.py:14
  102.9 1.4 %collective-permute-start.1 = (bf16[128,512]{1,0:T(8,128)(2,1)S(1)}, bf16[128,512]{1,0:T(8,128)(2,1)S(1)}, u32[]{:S(2)}, u32[]{:S(2)}) collective-permute-start(bf16[128,512]{1,0:T(8,128)(2,1)S(1)} %fusion.3), channel_id=1, source_target_pairs={{0,4},{4,0},{8,12},{12,8},{16,20},{20,16},{24,28},{28,24},{1,5},{5... | collective-permute-start | bytes 393224 | tf_op jit(solution)/shard_map/ppermute | solution.py:14
  104.3 8.4 %collective-permute-start.2 = (bf16[256,512]{1,0:T(8,128)(2,1)S(1)}, bf16[256,512]{1,0:T(8,128)(2,1)S(1)}, u32[]{:S(2)}, u32[]{:S(2)}) collective-permute-start(bf16[256,512]{1,0:T(8,128)(2,1)S(1)} %maximum_select_fusion.6), channel_id=1, source_target_pairs={{0,8},{8,0},{4,12},{12,4},{16,24},{24,16},{20,28},{28,20},{1,9},{9... | collective-permute-start | bytes 786440 | tf_op jit(solution)/shard_map/ppermute | solution.py:14
  113.0 1.3 %collective-permute-start.3 = (bf16[64,512]{1,0:T(8,128)(2,1)S(1)}, bf16[64,512]{1,0:T(8,128)(2,1)S(1)}, u32[]{:S(2)}, u32[]{:S(2)}) collective-permute-start(bf16[64,512]{1,0:T(8,128)(2,1)S(1)} %fusion.4), channel_id=1, source_target_pairs={{0,4},{4,0},{8,12},{12,8},{16,20},{20,16},{24,28},{28,24},{1,5},{5... | collective-permute-start | bytes 196616 | tf_op jit(solution)/shard_map/ppermute | solution.py:14
  114.4 5.6 %collective-permute-start.4 = (bf16[128,512]{1,0:T(8,128)(2,1)S(1)}, bf16[128,512]{1,0:T(8,128)(2,1)S(1)}, u32[]{:S(2)}, u32[]{:S(2)}) collective-permute-start(bf16[128,512]{1,0:T(8,128)(2,1)S(1)} %maximum_select_fusion.8), channel_id=1, source_target_pairs={{0,8},{8,0},{4,12},{12,4},{16,24},{24,16},{20,28},{28,20},{1,9},{9... | collective-permute-start | bytes 393224 | tf_op jit(solution)/shard_map/ppermute | solution.py:14
  120.1 7.6 %collective-permute-start.5 = (bf16[256,512]{1,0:T(8,128)(2,1)S(1)}, bf16[256,512]{1,0:T(8,128)(2,1)S(1)}, u32[]{:S(2)}, u32[]{:S(2)}) collective-permute-start(bf16[256,512]{1,0:T(8,128)(2,1)S(1)} %maximum_select_fusion.7), channel_id=1, source_target_pairs={{0,16},{16,0},{4,20},{20,4},{8,24},{24,8},{12,28},{28,12},{1,17},{... | collective-permute-start | bytes 786440 | tf_op jit(solution)/shard_map/ppermute | solution.py:14
where the time goes:
time: 130 us; the launch traced here: 129 us
  local copies, waits for them, and re-layouts  38 us (29%)
  blocking collectives  32 us (25%)
  waiting for transfers between devices  20.9 us (16%)
  matrix products  18.7 us (14%)
  other arithmetic  13.2 us (10%)
  starting transfers between devices  5.05 us (4%)
    all_to_all x1, blocking collectives, local(): lax.all_to_all(skeleton, 'rhs', split_axis=2, concat_axis=0, tiled=True)  32 us
    gather x1, local copies, waits for them, and re-layouts, pick_rows(): return block[chosen]  25.4 us
    ppermute x6, waiting for transfers between devices, partner(): return lax.ppermute(block, axis, route)  20.9 us
    unnamed x2, other arithmetic  12.4 us
    dot_general x4, matrix products, climb(): jnp.einsum('nij,njc->nic', matrices, stacked, preferred_element_type=jnp....  9.01 us
    dot_general x1, matrix products, local(): jnp.einsum('nsm,nmc->nsc', leaf_coef, points, preferred_element_type=jnp....  8.91 us
    unnamed x11, local copies, waits for them, and re-layouts  6.47 us
    ppermute x6, starting transfers between devices, partner(): return lax.ppermute(block, axis, route)  5.05 us
  transfers between devices with their start and end apart: 6, of which 6 were waited for; matrix products, arithmetic and copies ran while one was open for 0% of the time, Pallas kernels for 0%

commit v1 on v0

v1 whole, which is shorter than its diff:
```python
import functools

import jax
import jax.numpy as jnp
from jax import lax
from jax.experimental import pallas as pl
from jax.experimental.pallas import tpu as pltpu
from jax.sharding import PartitionSpec as P

PARTS = 2


def bit(value, k):
    return (value // (1 << k)) % 2


def flip(value, offset, bits):
    out = 0
    for k in range(bits):
        a, b = bit(value, k), bit(offset, k)
        out = out + (a + b - 2 * a * b) * (1 << k)
    return out


def dot(a, b):
    return jnp.dot(a, b, preferred_element_type=jnp.float32)


def kernel(plan, charges, coef, rows, interp, top, root_out, top_out, *scratch):
    (points, mats, picks, nodes, tops, mixed, first, arrived, merged, stacks,
     load_sem, send_sem, recv_sem, top_send, top_recv) = scratch
    R, L, H, cw = plan["R"], plan["L"], plan["H"], plan["cw"]
    leaves, S, M = plan["leaves"], plan["S"], plan["M"]
    m, n_leaf, early = plan["m"], plan["n_leaf"], plan["early"]
    total = leaves * R
    z = lax.axis_index("rhs")
    p = lax.axis_index("leaf")

    barrier = pltpu.get_barrier_semaphore()
    for b in range(m):
        pl.semaphore_signal(barrier, inc=1, device_id={"rhs": flip(z, 1 << b, m)},
                            device_id_type=pl.DeviceIdType.MESH)
    for delta in range(1, n_leaf):
        pl.semaphore_signal(barrier, inc=1, device_id={"leaf": flip(p, delta, L)},
                            device_id_type=pl.DeviceIdType.MESH)

    chunks = R * H

    def chunk_copy(i):
        column = (flip(z, R - 1 - i // H, m) * H + i % H) * cw
        return pltpu.make_async_copy(
            charges.at[:, pl.ds(pl.multiple_of(column, cw), cw)], points.at[i], load_sem.at[i])

    small = [(rows, picks)] + [(coef.at[n], mats.at[n, pl.ds(0, S)]) for n in range(leaves)]
    where = {}
    late = []
    for level in range(1, early + m + 1):
        count = max(leaves >> level, 1)
        if level <= early:
            start = total - (total >> level - 1) + z * count
        else:
            start = total - (total >> level - 1) + z // (1 << level - early)
        for k in range(count):
            where[level, k] = len(where)
            late.append((interp.at[start + k], nodes.at[where[level, k]]))
    late.append((top, tops))
    loads = [pltpu.make_async_copy(a, b, load_sem.at[chunks + i])
             for i, (a, b) in enumerate(small + late)]
    for copy in loads[:len(small)]:
        copy.start()
    chunk_copy(0).start()
    for copy in loads[len(small):]:
        copy.start()
    for i in range(1, chunks):
        chunk_copy(i).start()

    loads[0].wait()
    lanes = lax.broadcasted_iota(jnp.int32, (S, 128), 1)
    for n in range(leaves):
        across = jnp.transpose(jnp.broadcast_to(picks[n:n + 1, :], (128, S)))
        for t in range(M // 128):
            mats[n, S:, t * 128:(t + 1) * 128] = jnp.where(
                across == lanes + t * 128, 1.0, 0.0).astype(jnp.bfloat16)
    for copy in loads[1:]:
        copy.wait()
    pl.semaphore_wait(barrier, m + n_leaf - 1)

    order = sorted(
        [(b, d, h) for d in range(1, R) for h in range(H) for b in [(d & -d).bit_length() - 1]],
        key=lambda s: (-bin(s[1]).count("1"), s[2], -s[0]))
    slot = {s: i for i, s in enumerate(order)}

    def first_of(d, h):
        return (R - 1 - d) * H + h

    merge_keys = [(b, d, h) for b in range(1, m) for d in range(0, R, 1 << b) for h in range(H)]
    merge_at = {k: i for i, k in enumerate(merge_keys)}

    def held(b, d, h):
        return first.at[first_of(d, h)] if b == 0 else merged.at[merge_at[b, d, h]]

    def send(b, d, h):
        s = slot[b, d, h]
        return pltpu.make_async_remote_copy(
            src_ref=held(b, d, h), dst_ref=arrived.at[s], send_sem=send_sem.at[s],
            recv_sem=recv_sem.at[s], device_id={"rhs": flip(z, 1 << b, m)},
            device_id_type=pl.DeviceIdType.MESH)

    def chunk(i, carry):
        chunk_copy(i).wait()
        for n in range(leaves):
            both = dot(mats[n], points[i, n * M:(n + 1) * M, :])
            mixed[n * S:(n + 1) * S, :] = (both[:S] + both[S:]).astype(jnp.bfloat16)
        for level in range(1, early + 1):
            for k in range(leaves >> level):
                node = dot(nodes[where[level, k]], mixed[2 * k * S:(2 * k + 2) * S, :])
                mixed[k * S:(k + 1) * S, :] = node.astype(jnp.bfloat16)
        first[i] = mixed[:S, :]
        if m:
            for h in range(H):
                @pl.when(i == h)
                def _():
                    send(0, R - 1, h).start()
        return carry

    lax.fori_loop(0, chunks, chunk, 0)

    def merge(b, d, h):
        s = slot[b, d + (1 << b), h]
        send(b, d + (1 << b), h).wait_recv()
        matrix = where[early + b + 1, 0]
        own = bit(z, b)
        mine = nodes[matrix, :, pl.ds(pl.multiple_of(own * S, S), S)]
        other = nodes[matrix, :, pl.ds(pl.multiple_of((1 - own) * S, S), S)]
        return (dot(mine, held(b, d, h)[...]) + dot(other, arrived[s])).astype(jnp.bfloat16)

    done = set()

    def ready(b, d, h):
        if b == 0 or (b, d, h) in done:
            return
        ready(b - 1, d, h)
        merged[merge_at[b, d, h]] = merge(b - 1, d, h)
        done.add((b, d, h))

    for b, d, h in order:
        if d == R - 1:
            continue
        ready(b, d, h)
        send(b, d, h).start()

    def top_copy(level, delta, h):
        group = 1 << level
        height = S >> level - 1
        j = p % group
        mine = stacks.at[level - 1, h, pl.ds(pl.multiple_of(j * height, height), height)]
        index = (group - 2 + delta) * H + h
        return pltpu.make_async_remote_copy(
            src_ref=mine, dst_ref=mine, send_sem=top_send.at[index], recv_sem=top_recv.at[index],
            device_id={"leaf": flip(p, delta, L)}, device_id_type=pl.DeviceIdType.MESH)

    def put(level, h, value):
        height = S >> level - 1
        j = p % (1 << level)
        stacks[level - 1, h, pl.ds(pl.multiple_of(j * height, height), height), :] = value
        for delta in range(1, 1 << level):
            top_copy(level, delta, h).start()

    def begin(h):
        ready(m - 1, 0, h)
        root = merge(m - 1, 0, h) if m else held(0, 0, h)[...]
        root_out[:, h * cw:(h + 1) * cw] = root
        if L:
            put(1, h, root)

    def climb(level, h):
        for delta in range(1, 1 << level):
            top_copy(level, delta, h).wait_recv()
        offset, count = S - (S >> level - 1), S >> level
        value = dot(tops[offset:offset + count, :], stacks[level - 1, h]).astype(jnp.bfloat16)
        top_out[offset:offset + count, h * cw:(h + 1) * cw] = value
        if level < L:
            put(level + 1, h, value)

    for h in range(H):
        begin(h)
        for level in range(1, L + 1):
            climb(level, h)

    for s in order:
        send(*s).wait_send()
    for level in range(1, L + 1):
        for delta in range(1, 1 << level):
            for h in range(H):
                top_copy(level, delta, h).wait_send()


def local(charges, leaf_coef, leaf_rows, local_interp, top_interp):
    R, n_leaf = lax.axis_size("rhs"), lax.axis_size("leaf")
    leaves, S, M = leaf_coef.shape
    cols = charges.shape[1]
    m, L = R.bit_length() - 1, n_leaf.bit_length() - 1
    early = leaves.bit_length() - 1
    H = PARTS
    cw = cols // R // H
    plan = dict(R=R, L=L, H=H, cw=cw, leaves=leaves, S=S, M=M, m=m, n_leaf=n_leaf, early=early)
    node_count = leaves - 1 + m
    merge_count = max(sum(R >> b for b in range(1, m)) * H, 1)
    sends = max((R - 1) * H, 1)
    top_sends = max(sum((1 << l) - 1 for l in range(1, L + 1)), 1)
    top_slots = max(((1 << L) - 2 + (1 << L)) * H, 1)
    bf = jnp.bfloat16
    pack = top_interp.shape[0]
    any_spec = pl.BlockSpec(memory_space=pl.ANY)
    vmem = pl.BlockSpec(memory_space=pltpu.VMEM)
    return pl.pallas_call(
        functools.partial(kernel, plan),
        out_shape=(jax.ShapeDtypeStruct((S, cw * H), bf), jax.ShapeDtypeStruct((pack, cw * H), bf)),
        in_specs=[any_spec] * 5,
        out_specs=(vmem, vmem),
        scratch_shapes=[
            pltpu.VMEM((R * H, leaves * M, cw), bf),
            pltpu.VMEM((leaves, 2 * S, M), bf),
            pltpu.VMEM((leaves, S), jnp.int32),
            pltpu.VMEM((node_count, S, 2 * S), bf),
            pltpu.VMEM((pack, 2 * S), bf),
            pltpu.VMEM((leaves * S, cw), bf),
            pltpu.VMEM((R * H, S, cw), bf),
            pltpu.VMEM((sends, S, cw), bf),
            pltpu.VMEM((merge_count, S, cw), bf),
            pltpu.VMEM((max(L, 1), H, 2 * S, cw), bf),
            pltpu.SemaphoreType.DMA((R * H + 2 + leaves + node_count,)),
            pltpu.SemaphoreType.DMA((sends,)),
            pltpu.SemaphoreType.DMA((sends,)),
            pltpu.SemaphoreType.DMA((top_slots,)),
            pltpu.SemaphoreType.DMA((top_slots,)),
        ],
        compiler_params=pltpu.CompilerParams(collective_id=0, has_side_effects=True,
                                             vmem_limit_bytes=60 * 1024 * 1024),
    )(charges, leaf_coef, leaf_rows, local_interp, top_interp)


def solution(mesh):
    placed = (
        P(("leaf", "rhs"), None),
        P(("leaf", "rhs"), None, None),
        P(("leaf", "rhs"), None),
        P("leaf", None, None),
        P("leaf", None),
    )
    return jax.shard_map(
        local,
        mesh=mesh,
        in_specs=placed,
        out_specs=(P("leaf", "rhs"), P("leaf", "rhs")),
        check_vma=False,
    )
```

time: 130 us -> 51.8 us (0.40)
  Pallas kernels: 0 us -> 47.7 us
  local copies, waits for them, and re-layouts: 38 us -> 3.31 us
  blocking collectives: 32 us -> 0 us
  waiting for transfers between devices: 20.9 us -> 0 us
  matrix products: 18.7 us -> 0 us
  other arithmetic: 13.2 us -> 0 us
  starting transfers between devices: 5.05 us -> 0 us
    pallas_call x0 -> x1, Pallas kernels: none -> 47.7 us  [local(): pl.pallas_call(functools.partial(kernel, plan), out_shape=(jax.ShapeDtype...]
    all_to_all x1 -> x0, blocking collectives: 32 us -> none  [local(): lax.all_to_all(skeleton, 'rhs', split_axis=2, concat_axis=0, tiled=True)]
    gather x1 -> x0, local copies, waits for them, and re-layouts: 25.4 us -> none  [pick_rows(): return block[chosen]]
    ppermute x6 -> x0, waiting for transfers between devices: 20.9 us -> none  [partner(): return lax.ppermute(block, axis, route)]
    dot_general x8 -> x0, matrix products: 18.7 us -> none  [the longest x4 9.01 us: climb(): jnp.einsum('nij,njc->nic', matrices, stacked, preferred_element_type=jnp....]
    unnamed x2 -> x0, other arithmetic: 12.4 us -> none
    ppermute x6 -> x0, starting transfers between devices: 5.05 us -> none  [partner(): return lax.ppermute(block, axis, route)]
    convert_element_type x1 -> x0, local copies, waits for them, and re-layouts: 4.6 us -> none  [climb(): return jnp.einsum('nij,njc->nic', matrices, stacked, preferred_element_ty...]
  transfers between devices with their start and end apart: 6 -> 0, of which waited for: 6 -> 0; matrix products, arithmetic and copies ran while one was open for 0% -> 0% of each run, Pallas kernels for 0% -> 0%
where the time goes in v1:
time: 51.8 us; the launch traced here: 51.6 us
  Pallas kernels  47.7 us (92%)
  local copies, waits for them, and re-layouts  3.31 us (6%)
  between operations  0.64 us (1%)
    pallas_call x1, Pallas kernels, local(): pl.pallas_call(functools.partial(kernel, plan), out_shape=(jax.ShapeDtype...  47.7 us
    unnamed x2, local copies, waits for them, and re-layouts  3.31 us

profile of v1, /device:TPU:0, one launch (start us, length us, event | category | flops | bytes accessed | tf_op | source)
XLA Modules:
  0.0 51.6 jit_solution(2890449965088502267)
XLA Ops:
  0.6 47.7 %shard_map.68 = (bf16[256,512]{1,0:T(8,128)(2,1)}, bf16[224,512]{1,0:T(8,128)(2,1)}) custom-call(bf16[2048,2048]{1,0:T(8,128)(2,1)} %charges.1, bf16[4,256,512]{2,1,0:T(8,128)(2,1)} %coef.1, s32[4,256]{1,0:T(4,128)} %rows.1, bf16[15,256,512]{2,1,0:T(8,128)(2,1)} %interp.1, bf16[224,512]{1,0:T(8,128)(2,1)} %top.1), custom_call_target="tpu_custom_call" | custom-call | tf_op jit(solution)/shard_map/pallas_call | solution.py:216
  48.3 1.7 %copy.9 = bf16[256,512]{1,0:T(8,128)(2,1)} copy(bf16[256,512]{1,0:T(8,128)(2,1)} %get-tuple-element.4) | data formatting | bytes 524288
  50.0 1.6 %copy.10 = bf16[224,512]{1,0:T(8,128)(2,1)} copy(bf16[224,512]{1,0:T(8,128)(2,1)} %get-tuple-element.5) | data formatting | bytes 458752

commit v2 on v1

--- a/solution.py
+++ b/solution.py
@@ -27,8 +27,10 @@
 
 
 def kernel(plan, charges, coef, rows, interp, top, root_out, top_out, *scratch):
-    (points, mats, picks, nodes, tops, mixed, first, arrived, merged, stacks,
-     load_sem, send_sem, recv_sem, top_send, top_recv) = scratch
+    (points, mats, picks, nodes, tops, mixed, first, arrived, merged,
+     tables, pairs, leaving, coming, padded, load_sem, send_sem, recv_sem,
+     table_send, table_recv, pair_send, pair_recv, part_send, part_recv) = scratch
+    pack = top.shape[0]
     R, L, H, cw = plan["R"], plan["L"], plan["H"], plan["cw"]
     leaves, S, M = plan["leaves"], plan["S"], plan["M"]
     m, n_leaf, early = plan["m"], plan["n_leaf"], plan["early"]
@@ -45,6 +47,16 @@
                             device_id_type=pl.DeviceIdType.MESH)
 
     chunks = R * H
+    fetches = [1] * (L > 0) + list(range(2, n_leaf, 2))
+
+    def table_copy(delta):
+        part = pl.ds(0, S // 2) if delta == 1 else pl.ds(S // 2, pack - S // 2)
+        k = fetches.index(delta)
+        return pltpu.make_async_remote_copy(
+            src_ref=top.at[part], dst_ref=tables.at[k, part], send_sem=table_send.at[k],
+            recv_sem=table_recv.at[k], device_id={"leaf": flip(p, delta, L)},
+            device_id_type=pl.DeviceIdType.MESH)
+
 
     def chunk_copy(i):
         column = (flip(z, R - 1 - i // H, m) * H + i % H) * cw
@@ -69,10 +81,9 @@
     for copy in loads[:len(small)]:
         copy.start()
     chunk_copy(0).start()
-    for copy in loads[len(small):]:
+    soon = len(small) + leaves - 1
+    for copy in loads[len(small):soon]:
         copy.start()
-    for i in range(1, chunks):
-        chunk_copy(i).start()
 
     loads[0].wait()
     lanes = lax.broadcasted_iota(jnp.int32, (S, 128), 1)
@@ -81,9 +92,15 @@
         for t in range(M // 128):
             mats[n, S:, t * 128:(t + 1) * 128] = jnp.where(
                 across == lanes + t * 128, 1.0, 0.0).astype(jnp.bfloat16)
-    for copy in loads[1:]:
+    for i in range(1, chunks):
+        chunk_copy(i).start()
+    for copy in loads[soon:]:
+        copy.start()
+    pl.semaphore_wait(barrier, m + n_leaf - 1)
+    for delta in fetches:
+        table_copy(delta).start()
+    for copy in loads[1:soon]:
         copy.wait()
-    pl.semaphore_wait(barrier, m + n_leaf - 1)
 
     order = sorted(
         [(b, d, h) for d in range(1, R) for h in range(H) for b in [(d & -d).bit_length() - 1]],
@@ -124,6 +141,8 @@
         return carry
 
     lax.fori_loop(0, chunks, chunk, 0)
+    for copy in loads[soon:-1]:
+        copy.wait()
 
     def merge(b, d, h):
         s = slot[b, d + (1 << b), h]
@@ -149,22 +168,27 @@
         ready(b, d, h)
         send(b, d, h).start()
 
-    def top_copy(level, delta, h):
-        group = 1 << level
+    def pair_copy(level, h):
         height = S >> level - 1
-        j = p % group
-        mine = stacks.at[level - 1, h, pl.ds(pl.multiple_of(j * height, height), height)]
-        index = (group - 2 + delta) * H + h
+        mine = pairs.at[level - 1, h, pl.ds(pl.multiple_of(p % 2 * height, height), height)]
         return pltpu.make_async_remote_copy(
-            src_ref=mine, dst_ref=mine, send_sem=top_send.at[index], recv_sem=top_recv.at[index],
+            src_ref=mine, dst_ref=mine, send_sem=pair_send.at[level - 1, h],
+            recv_sem=pair_recv.at[level - 1, h], device_id={"leaf": flip(p, 1, L)},
+            device_id_type=pl.DeviceIdType.MESH)
+
+    def part_copy(level, delta, h):
+        i = delta // 2
+        height = S >> level
+        return pltpu.make_async_remote_copy(
+            src_ref=leaving.at[level - 1, i, h, pl.ds(0, height)],
+            dst_ref=coming.at[level - 1, i, h, pl.ds(0, height)],
+            send_sem=part_send.at[level - 1, i, h], recv_sem=part_recv.at[level - 1, i, h],
             device_id={"leaf": flip(p, delta, L)}, device_id_type=pl.DeviceIdType.MESH)
 
     def put(level, h, value):
         height = S >> level - 1
-        j = p % (1 << level)
-        stacks[level - 1, h, pl.ds(pl.multiple_of(j * height, height), height), :] = value
-        for delta in range(1, 1 << level):
-            top_copy(level, delta, h).start()
+        pairs[level - 1, h, pl.ds(pl.multiple_of(p % 2 * height, height), height), :] = value
+        pair_copy(level, h).start()
 
     def begin(h):
         ready(m - 1, 0, h)
@@ -173,26 +197,66 @@
         if L:
             put(1, h, root)
 
+    def share(level, matrix, h):
+        width = 2 * (S >> level - 1)
+        chip = p % (1 << level) // 2
+        rows = slice(S - (S >> level - 1), S - (S >> level))
+        if width % 128 == 0:
+            columns = pl.ds(pl.multiple_of(chip * width, width), width)
+            return dot(matrix[rows, columns], pairs[level - 1, h, :width, :])
+        padded[...] = jnp.zeros_like(padded)
+        padded[pl.ds(pl.multiple_of(chip * width, width), width), :] = pairs[level - 1, h, :width, :]
+        return dot(matrix[rows, :], padded[...])
+
     def climb(level, h):
-        for delta in range(1, 1 << level):
-            top_copy(level, delta, h).wait_recv()
         offset, count = S - (S >> level - 1), S >> level
-        value = dot(tops[offset:offset + count, :], stacks[level - 1, h]).astype(jnp.bfloat16)
+        if level != 2:
+            pair_copy(level, h).wait_recv()
+        if level > 1:
+            for delta in range(2, 1 << level, 2):
+                leaving[level - 1, delta // 2, h, :count, :] = share(
+                    level, tables.at[fetches.index(delta)], h).astype(jnp.bfloat16)
+                part_copy(level, delta, h).start()
+        value = share(level, tops, h)
+        if level == 1 and L > 1:
+            other = share(1, tables.at[0], h)
+            pairs[1, h, pl.ds(pl.multiple_of((1 - p % 2) * count, count), count), :] = other.astype(jnp.bfloat16)
+            pairs[1, h, pl.ds(pl.multiple_of(p % 2 * count, count), count), :] = value.astype(jnp.bfloat16)
+        return value
+
+    def finish(level, h, value):
+        offset, count = S - (S >> level - 1), S >> level
+        for delta in range(2, 1 << level, 2):
+            part_copy(level, delta, h).wait_recv()
+            value = value + coming[level - 1, delta // 2, h, :count, :].astype(jnp.float32)
+        value = value.astype(jnp.bfloat16)
+        if 2 <= level < L:
+            put(level + 1, h, value)
         top_out[offset:offset + count, h * cw:(h + 1) * cw] = value
-        if level < L:
-            put(level + 1, h, value)
 
     for h in range(H):
         begin(h)
-        for level in range(1, L + 1):
-            climb(level, h)
+    loads[-1].wait()
+    for level in range(1, L + 1):
+        if level == 1:
+            table_copy(1).wait_recv()
+        if level == 2:
+            for delta in fetches[1:]:
+                table_copy(delta).wait_recv()
+        values = [climb(level, h) for h in range(H)]
+        for h in range(H):
+            finish(level, h, values[h])
 
     for s in order:
         send(*s).wait_send()
+    for delta in fetches:
+        table_copy(delta).wait_send()
     for level in range(1, L + 1):
-        for delta in range(1, 1 << level):
-            for h in range(H):
-                top_copy(level, delta, h).wait_send()
+        for h in range(H):
+            if level != 2:
+                pair_copy(level, h).wait_send()
+            for delta in range(2, 1 << level, 2):
+                part_copy(level, delta, h).wait_send()
 
 
 def local(charges, leaf_coef, leaf_rows, local_interp, top_interp):
@@ -207,8 +271,7 @@
     node_count = leaves - 1 + m
     merge_count = max(sum(R >> b for b in range(1, m)) * H, 1)
     sends = max((R - 1) * H, 1)
-    top_sends = max(sum((1 << l) - 1 for l in range(1, L + 1)), 1)
-    top_slots = max(((1 << L) - 2 + (1 << L)) * H, 1)
+    top_levels, chips = max(L, 1), max(n_leaf // 2, 1)
     bf = jnp.bfloat16
     pack = top_interp.shape[0]
     any_spec = pl.BlockSpec(memory_space=pl.ANY)
@@ -228,12 +291,20 @@
             pltpu.VMEM((R * H, S, cw), bf),
             pltpu.VMEM((sends, S, cw), bf),
             pltpu.VMEM((merge_count, S, cw), bf),
-            pltpu.VMEM((max(L, 1), H, 2 * S, cw), bf),
+            pltpu.VMEM((max(n_leaf // 2, 1), pack, 2 * S), bf),
+            pltpu.VMEM((top_levels, H, 2 * S, cw), bf),
+            pltpu.VMEM((top_levels, chips, H, S // 4, cw), bf),
+            pltpu.VMEM((top_levels, chips, H, S // 4, cw), bf),
+            pltpu.VMEM((2 * S, cw), bf),
             pltpu.SemaphoreType.DMA((R * H + 2 + leaves + node_count,)),
             pltpu.SemaphoreType.DMA((sends,)),
             pltpu.SemaphoreType.DMA((sends,)),
-            pltpu.SemaphoreType.DMA((top_slots,)),
-            pltpu.SemaphoreType.DMA((top_slots,)),
+            pltpu.SemaphoreType.DMA((max(n_leaf // 2, 1),)),
+            pltpu.SemaphoreType.DMA((max(n_leaf // 2, 1),)),
+            pltpu.SemaphoreType.DMA((top_levels, H)),
+            pltpu.SemaphoreType.DMA((top_levels, H)),
+            pltpu.SemaphoreType.DMA((top_levels, chips, H)),
+            pltpu.SemaphoreType.DMA((top_levels, chips, H)),
         ],
         compiler_params=pltpu.CompilerParams(collective_id=0, has_side_effects=True,
                                              vmem_limit_bytes=60 * 1024 * 1024),

time: 51.8 us -> 43.5 us (0.84)
  Pallas kernels: 47.7 us -> 39.4 us
    pallas_call x1, Pallas kernels: 47.7 us -> 39.4 us  [local(): pl.pallas_call(functools.partial(kernel, plan), out_shape=(jax.ShapeDtype...]
where the time goes in v2:
time: 43.5 us; the launch traced here: 43.3 us
  Pallas kernels  39.4 us (91%)
  local copies, waits for them, and re-layouts  3.31 us (8%)
  between operations  0.64 us (1%)
    pallas_call x1, Pallas kernels, local(): pl.pallas_call(functools.partial(kernel, plan), out_shape=(jax.ShapeDtype...  39.4 us
    unnamed x2, local copies, waits for them, and re-layouts  3.31 us

profile of v2, /device:TPU:0, one launch (start us, length us, event | category | flops | bytes accessed | tf_op | source)
XLA Modules:
  0.0 43.3 jit_solution(15198581455259734529)
XLA Ops:
  0.6 39.4 %shard_map.68 = (bf16[256,512]{1,0:T(8,128)(2,1)}, bf16[224,512]{1,0:T(8,128)(2,1)}) custom-call(bf16[2048,2048]{1,0:T(8,128)(2,1)} %charges.1, bf16[4,256,512]{2,1,0:T(8,128)(2,1)} %coef.1, s32[4,256]{1,0:T(4,128)} %rows.1, bf16[15,256,512]{2,1,0:T(8,128)(2,1)} %interp.1, bf16[224,512]{1,0:T(8,128)(2,1)} %top.1), custom_call_target="tpu_custom_call" | custom-call | tf_op jit(solution)/shard_map/pallas_call | solution.py:279
  40.0 1.7 %copy.9 = bf16[256,512]{1,0:T(8,128)(2,1)} copy(bf16[256,512]{1,0:T(8,128)(2,1)} %get-tuple-element.4) | data formatting | bytes 524288
  41.7 1.6 %copy.10 = bf16[224,512]{1,0:T(8,128)(2,1)} copy(bf16[224,512]{1,0:T(8,128)(2,1)} %get-tuple-element.5) | data formatting | bytes 458752

commit v3 on v2

--- a/solution.py
+++ b/solution.py
@@ -47,6 +47,10 @@
                             device_id_type=pl.DeviceIdType.MESH)
 
     chunks = R * H
+    order = sorted(
+        [(b, d, h) for d in range(1, R) for h in range(H) for b in [(d & -d).bit_length() - 1]],
+        key=lambda s: (-bin(s[1]).count("1"), s[2], s[0]))
+    places = [(d, h) for _, d, h in order] + [(0, h) for h in range(H)]
     fetches = [1] * (L > 0) + list(range(2, n_leaf, 2))
 
     def table_copy(delta):
@@ -59,7 +63,8 @@
 
 
     def chunk_copy(i):
-        column = (flip(z, R - 1 - i // H, m) * H + i % H) * cw
+        d, h = places[i]
+        column = (flip(z, d, m) * H + h) * cw
         return pltpu.make_async_copy(
             charges.at[:, pl.ds(pl.multiple_of(column, cw), cw)], points.at[i], load_sem.at[i])
 
@@ -102,13 +107,10 @@
     for copy in loads[1:soon]:
         copy.wait()
 
-    order = sorted(
-        [(b, d, h) for d in range(1, R) for h in range(H) for b in [(d & -d).bit_length() - 1]],
-        key=lambda s: (-bin(s[1]).count("1"), s[2], -s[0]))
     slot = {s: i for i, s in enumerate(order)}
 
     def first_of(d, h):
-        return (R - 1 - d) * H + h
+        return places.index((d, h))
 
     merge_keys = [(b, d, h) for b in range(1, m) for d in range(0, R, 1 << b) for h in range(H)]
     merge_at = {k: i for i, k in enumerate(merge_keys)}
@@ -123,7 +125,7 @@
             recv_sem=recv_sem.at[s], device_id={"rhs": flip(z, 1 << b, m)},
             device_id_type=pl.DeviceIdType.MESH)
 
-    def chunk(i, carry):
+    def chunk(i):
         chunk_copy(i).wait()
         for n in range(leaves):
             both = dot(mats[n], points[i, n * M:(n + 1) * M, :])
@@ -133,16 +135,6 @@
                 node = dot(nodes[where[level, k]], mixed[2 * k * S:(2 * k + 2) * S, :])
                 mixed[k * S:(k + 1) * S, :] = node.astype(jnp.bfloat16)
         first[i] = mixed[:S, :]
-        if m:
-            for h in range(H):
-                @pl.when(i == h)
-                def _():
-                    send(0, R - 1, h).start()
-        return carry
-
-    lax.fori_loop(0, chunks, chunk, 0)
-    for copy in loads[soon:-1]:
-        copy.wait()
 
     def merge(b, d, h):
         s = slot[b, d + (1 << b), h]
@@ -162,11 +154,18 @@
         merged[merge_at[b, d, h]] = merge(b - 1, d, h)
         done.add((b, d, h))
 
-    for b, d, h in order:
-        if d == R - 1:
-            continue
+    for i, (b, d, h) in enumerate(order):
+        chunk(i)
+        if b and not done:
+            for copy in loads[soon:-1]:
+                copy.wait()
         ready(b, d, h)
         send(b, d, h).start()
+    for i in range(len(order), chunks):
+        chunk(i)
+    if m < 2:
+        for copy in loads[soon:-1]:
+            copy.wait()
 
     def pair_copy(level, h):
         height = S >> level - 1
@@ -257,6 +256,15 @@
                 pair_copy(level, h).wait_send()
             for delta in range(2, 1 << level, 2):
                 part_copy(level, delta, h).wait_send()
+
+
+def store(root, top, root_out, top_out, sems):
+    copies = [pltpu.make_async_copy(root, root_out, sems.at[0]),
+              pltpu.make_async_copy(top, top_out, sems.at[1])]
+    for copy in copies:
+        copy.start()
+    for copy in copies:
+        copy.wait()
 
 
 def local(charges, leaf_coef, leaf_rows, local_interp, top_interp):
@@ -276,7 +284,7 @@
     pack = top_interp.shape[0]
     any_spec = pl.BlockSpec(memory_space=pl.ANY)
     vmem = pl.BlockSpec(memory_space=pltpu.VMEM)
-    return pl.pallas_call(
+    results = pl.pallas_call(
         functools.partial(kernel, plan),
         out_shape=(jax.ShapeDtypeStruct((S, cw * H), bf), jax.ShapeDtypeStruct((pack, cw * H), bf)),
         in_specs=[any_spec] * 5,
@@ -309,6 +317,13 @@
         compiler_params=pltpu.CompilerParams(collective_id=0, has_side_effects=True,
                                              vmem_limit_bytes=60 * 1024 * 1024),
     )(charges, leaf_coef, leaf_rows, local_interp, top_interp)
+    return pl.pallas_call(
+        store,
+        out_shape=(jax.ShapeDtypeStruct((S, cw * H), bf), jax.ShapeDtypeStruct((pack, cw * H), bf)),
+        in_specs=[vmem, vmem],
+        out_specs=(any_spec, any_spec),
+        scratch_shapes=[pltpu.SemaphoreType.DMA((2,))],
+    )(*results)
 
 
 def solution(mesh):

time: 43.5 us -> 38.8 us (0.89)
  local copies, waits for them, and re-layouts: 3.31 us -> 0 us
  Pallas kernels: 39.4 us -> 37.9 us
    unnamed x2 -> x0, local copies, waits for them, and re-layouts: 3.31 us -> none
    pallas_call x1, Pallas kernels: 39.4 us -> 36.1 us  [local(): pl.pallas_call(functools.partial(kernel, plan), out_shape=(jax.ShapeDtype...]
    pallas_call x0 -> x1, Pallas kernels: none -> 1.81 us  [local(): pl.pallas_call(store, out_shape=(jax.ShapeDtypeStruct((S, cw * H), bf), j...]
where the time goes in v3:
time: 38.8 us; the launch traced here: 38.6 us
  Pallas kernels  37.9 us (98%)
  between operations  0.64 us (2%)
    pallas_call x1, Pallas kernels, local(): pl.pallas_call(functools.partial(kernel, plan), out_shape=(jax.ShapeDtype...  36.1 us
    pallas_call x1, Pallas kernels, local(): pl.pallas_call(store, out_shape=(jax.ShapeDtypeStruct((S, cw * H), bf), j...  1.81 us

profile of v3, /device:TPU:0, one launch (start us, length us, event | category | flops | bytes accessed | tf_op | source)
XLA Modules:
  0.0 38.6 jit_solution(14366360677707495487)
XLA Ops:
  0.6 36.1 %shard_map.68 = (bf16[256,512]{1,0:T(8,128)(2,1)}, bf16[224,512]{1,0:T(8,128)(2,1)}) custom-call(bf16[2048,2048]{1,0:T(8,128)(2,1)} %charges.1, bf16[4,256,512]{2,1,0:T(8,128)(2,1)} %coef.1, s32[4,256]{1,0:T(4,128)} %rows.1, bf16[15,256,512]{2,1,0:T(8,128)(2,1)} %interp.1, bf16[224,512]{1,0:T(8,128)(2,1)} %top.1), custom_call_target="tpu_custom_call" | custom-call | tf_op jit(solution)/shard_map/pallas_call | solution.py:287
  36.8 1.8 %shard_map.69 = (bf16[256,512]{1,0:T(8,128)(2,1)}, bf16[224,512]{1,0:T(8,128)(2,1)}) custom-call(bf16[256,512]{1,0:T(8,128)(2,1)} %get-tuple-element.4.root, bf16[224,512]{1,0:T(8,128)(2,1)} %get-tuple-element.5.top), custom_call_target="tpu_custom_call" | custom-call | tf_op jit(solution)/shard_map/pallas_call | solution.py:320
